TPU v7x, 32 devices: a whole 2x2x4 slice. The times are simulated.
32 devices in a mesh: row: 4 (over y, x), col: 8 (over z, core).
Axes of the slice: x: 2, y: 2, z: 4, core: 2. Of those that a mesh axis runs over, the one named last changes fastest.
Arguments:
- pair_rep: bfloat16 [512, 512, 128], P('row', 'col'), may hold values from -6 to 6
- ln_gain: float32 [128], replicated, may hold values from 0.1 to 1.9
- ln_shift: float32 [128], replicated, may hold values from -3 to 3
- w_proj: bfloat16 [128, 512], replicated, may hold values from -0.5 to 0.5
- gate_bias: float32 [128], replicated, may hold values from -4 to 4
- w_bias: bfloat16 [128, 4], replicated, may hold values from -11 to 11
- w_out: bfloat16 [128, 128], replicated, may hold values from -0.5 to 0.5
- out_bias: float32 [128], replicated, may hold values from -3 to 3
- block_valid: int32 [4], replicated, may hold values from 0 to 1, as said below
Outputs:
- pair_out: bfloat16 [512, 512, 128], P('row', 'col')
Inputs may be any that keep to these rules, and one draw needn't show every extreme that they name: block_valid[b] is 1 when residues b * 128 to (b + 1) * 128 - 1 are present and 0 when they are padding; blocks 0 and 2 are always present, and at least one other block is always padding.
All inputs are finite; a program needn't handle non-finite values.
Results may differ from a plain program's by a relative error of at most 0.0082.
Values may be sent and summed in bfloat16 or wider, within the bound.
A program may use at most 192 MiB of HBM per device.

v0:
```python
import math

import jax
import jax.numpy as jnp
from jax import lax
from jax.sharding import PartitionSpec as P

H = 4
HD = 32
BLK = 128


def layer_norm(values, ln_gain, ln_shift):
    widened = values.astype(jnp.float32)
    average = jnp.mean(widened, axis=-1, keepdims=True)
    spread = jnp.mean((widened - average) ** 2, axis=-1, keepdims=True)
    return ((widened - average) * lax.rsqrt(spread + 1e-05) * ln_gain + ln_shift).astype(
        jnp.bfloat16
    )


def residue_valid(block_valid, residues):
    blocks = block_valid.shape[0]
    block_width = residues // blocks
    owner = jnp.arange(residues, dtype=jnp.int32) // block_width
    matches = (owner[:, None] == jnp.arange(blocks, dtype=jnp.int32)[None, :]).astype(jnp.float32)
    return jnp.sum(matches * block_valid.astype(jnp.float32)[None, :], axis=1)


def start_state(width_j, query_count):
    running_max = jnp.full((H, width_j, query_count), -1e30, jnp.float32)
    denominator = jnp.zeros((H, width_j, query_count), jnp.float32)
    weighted = jnp.zeros((query_count, width_j, H, HD), jnp.float32)
    return (running_max, denominator, weighted)


def finish(carried):
    running_max, denominator, weighted = carried
    mixed = weighted / jnp.transpose(denominator, (2, 1, 0))[..., None]
    return mixed.reshape(mixed.shape[0], mixed.shape[1], H * HD).astype(jnp.bfloat16)


def fold_keys(carried, queries, key_rows, values, bias_part, validity):
    query_count, width_j, inner = queries.shape
    key_count = key_rows.shape[0]
    key_step = math.gcd(key_count, BLK)
    steps = key_count // key_step
    query_heads = queries.reshape(query_count, width_j, H, HD)
    key_blocks = key_rows.reshape(steps, key_step, width_j, H, HD)
    value_blocks = values.reshape(steps, key_step, width_j, H, HD)
    bias_blocks = jnp.transpose(bias_part.reshape(H, query_count, steps, key_step), (2, 0, 1, 3))
    mask_blocks = validity.reshape(steps, key_step)

    def update(carried_in, operands):
        key_part, value_part, bias_block, mask_part = operands
        running_max, denominator, weighted = carried_in
        scores = jnp.einsum(
            "ijhd,kjhd->hjik", query_heads, key_part, preferred_element_type=jnp.float32
        )
        scores = scores + bias_block[:, None, :, :]
        scores = jnp.where(mask_part[None, None, None, :] > 0, scores, jnp.float32(-1e30))
        renewed = jnp.maximum(running_max, jnp.max(scores, axis=-1))
        weights = jnp.exp(scores - renewed[..., None]) * mask_part[None, None, None, :]
        shrink = jnp.exp(running_max - renewed)
        denominator = denominator * shrink + jnp.sum(weights, axis=-1)
        product = jnp.einsum(
            "hjik,kjhd->ijhd",
            weights.astype(jnp.bfloat16),
            value_part,
            preferred_element_type=jnp.float32,
        )
        weighted = weighted * jnp.transpose(shrink, (2, 1, 0))[..., None] + product
        return (renewed, denominator, weighted)

    def scan_step(carried_in, operands):
        renewed = lax.cond(
            jnp.max(operands[3]) > 0, update, lambda kept, ignored: kept, carried_in, operands
        )
        return (renewed, None)

    result, ignored = lax.scan(
        scan_step, carried, (key_blocks, value_blocks, bias_blocks, mask_blocks)
    )
    return result


def shards(pair_rep, ln_gain, ln_shift, w_proj, gate_bias, w_bias, w_out, out_bias, block_valid):
    rows_dev, cols_dev, channels = pair_rep.shape
    row_count = lax.axis_size("row")
    row_id = lax.axis_index("row")
    col_id = lax.axis_index("col")
    residues = rows_dev * row_count
    inner = H * HD
    query_scale = HD ** (-0.5)
    validity = residue_valid(block_valid, residues)
    normed = layer_norm(pair_rep, ln_gain, ln_shift)
    flat_rows = normed.reshape(rows_dev * cols_dev, channels)
    bias_local = jnp.dot(flat_rows, w_bias, preferred_element_type=jnp.float32)
    bias_local = jnp.transpose(bias_local.reshape(rows_dev, cols_dev, H), (2, 1, 0))
    bias_cols = lax.all_gather(bias_local, "row", axis=2, tiled=True)
    regrouped = lax.all_to_all(normed, "row", split_axis=1, concat_axis=0, tiled=True)
    width_j = regrouped.shape[1]
    projected = jnp.dot(
        regrouped.reshape(residues * width_j, channels),
        w_proj[:, : 3 * inner],
        preferred_element_type=jnp.float32,
    )
    projected = projected.reshape(residues, width_j, 3 * inner)
    queries = (projected[..., :inner] * query_scale).astype(jnp.bfloat16)
    key_rows = projected[..., inner : 2 * inner].astype(jnp.bfloat16)
    values = projected[..., 2 * inner :].astype(jnp.bfloat16)
    bias_piece = lax.all_gather(bias_cols, "col", axis=1, tiled=True)
    span_rows = bias_piece.shape[1]
    query_block = math.gcd(span_rows, cols_dev)
    block_count = span_rows // query_block
    query_rows = queries
    query_rows = query_rows.reshape(block_count, query_block, width_j, inner)
    bias_blocks = jnp.transpose(
        bias_piece.reshape(H, block_count, query_block, residues), (1, 0, 2, 3)
    )

    def one_block(operands):
        query_part, bias_part = operands
        carried = fold_keys(
            start_state(width_j, query_block), query_part, key_rows, values, bias_part, validity
        )
        return finish(carried)

    results = lax.map(one_block, (query_rows, bias_blocks))
    gathered = results.reshape(span_rows, width_j, inner)
    attended = lax.all_to_all(gathered, "row", split_axis=0, concat_axis=1, tiled=True)
    gate_pre = jnp.dot(flat_rows, w_proj[:, 3 * inner :], preferred_element_type=jnp.float32)
    gate_pre = gate_pre.reshape(rows_dev, cols_dev, inner)
    gate_act = jax.nn.sigmoid(gate_pre + gate_bias)
    gated_rows = (gate_act * attended.astype(jnp.float32)).astype(jnp.bfloat16)
    update = jnp.dot(
        gated_rows.reshape(rows_dev * cols_dev, inner), w_out, preferred_element_type=jnp.float32
    )
    update = update.reshape(rows_dev, cols_dev, channels) + out_bias
    row_valid = lax.dynamic_slice_in_dim(validity, row_id * rows_dev, rows_dev, 0)
    col_valid = lax.dynamic_slice_in_dim(validity, col_id * cols_dev, cols_dev, 0)
    pair_mask = row_valid[:, None] * col_valid[None, :]
    return (pair_rep.astype(jnp.float32) + update * pair_mask[..., None]).astype(jnp.bfloat16)


def solution(mesh):
    return jax.shard_map(
        shards,
        mesh=mesh,
        in_specs=(P("row", "col", None), P(), P(), P(), P(), P(), P(), P(), P()),
        out_specs=P("row", "col", None),
        check_vma=False,
    )
```

profile of v0, /device:TPU:0, one launch (start us, length us, event | category | flops | bytes accessed | tf_op | source)
XLA Modules:
  0.0 400.0 jit_solution(1915389312735172597)
XLA Ops:
  6.6 3.5 convert_reduce_fusion
  10.1 6.1 %fusion.16 = f32[128,64]{0,1:T(8,128)S(1)} fusion(f32[128,64]{0,1:T(8,128)S(1)} %broadcast_multiply_fusion.1, bf16[128,64,128]{2,1,0:T(8,128)(2,1)S(1)} %copy-done.1), kind=kLoop, calls=%fused_computation.31 | loop fusion | flops 4186112 | bytes 2162688 | tf_op jit(solution)/shard_map/reduce_sum | solution.py:16
  16.3 5.0 %fusion.19 = bf16[128,64,128]{2,0,1:T(8,128)(2,1)S(1)} fusion(f32[128]{0:T(128)S(1)} %copy-done.7, f32[128]{0:T(128)S(1)} %copy-done.8, f32[128,64]{0,1:T(8,128)S(1)} %add_rsqrt_fusion, f32[128,64]{0,1:T(8,128)S(1)} %broadcast_multiply_fusion.1, bf16[128,64,128]{2,1,0:T(8,128)(2,1)S(1)} %copy-done.1), kind=kLoop, calls=%fused_computation.34 | loop fusion | flops 6291456 | bytes 4260864 | tf_op jit(solution)/shard_map/convert_element_type | solution.py:17
  23.2 12.3 %all_gather.6 = f32[4,64,512]{2,0,1:T(4,128)} all-gather(f32[4,64,128]{2,0,1:T(4,128)S(1)} %convolution_bitcast_fusion.1), channel_id=1, replica_groups=mesh['row'=4,'col'=8] {'row'}, dimensions={2}, use_global_device_ids=true | all-gather | bytes 655360 | tf_op jit(solution)/shard_map/all_gather | solution.py:100
  35.5 3.8 all-to-all-start
  39.4 23.1 %all-to-all-done = bf16[128,64,128]{2,0,1:T(8,128)(2,1)S(1)} async-done(((bf16[128,64,128]{2,0,1:T(8,128)(2,1)}), bf16[128,64,128]{2,0,1:T(8,128)(2,1)S(1)}, u32[]{:S(2)}, u32[]{:S(2)}) %all-to-all-start) | async-done | bytes 2097184 | tf_op jit(solution)/shard_map/all_to_all | solution.py:101
  63.4 6.3 %fusion.38 = (bf16[512,16,384]{2,0,1:T(8,128)(2,1)S(1)}, f32[512,16,384]{2,0,1:T(8,128)}) fusion(bf16[512,16,128]{2,0,1:T(8,128)(2,1)S(1)} %bitcast.98, bf16[128,512]{1,0:T(8,128)(2,1)S(1)} %copy-done.5), kind=kOutput, calls=%fused_computation.65 | convolution fusion | flops 808452096 | bytes 21069824 | tf_op jit(solution)/shard_map/dot_general | solution.py:103
  78.1 3.9 copy.80
  82.0 4.0 reshape.132
  86.0 4.2 %fusion.21 = bf16[512,16,128]{2,0,1:T(8,128)(2,1)} fusion(f32[512,16,384]{2,0,1:T(8,128)} %get-tuple-element.295), kind=kLoop, calls=%fused_computation.37 | loop fusion | flops 2097152 | bytes 6291456 | tf_op jit(solution)/shard_map/convert_element_type | solution.py:109
  90.2 5.4 %copy.101 = f32[4,8,64,512]{3,2,0,1:T(8,128)} copy(f32[4,8,64,512]{3,0,2,1:T(4,128)} %bitcast.100) | data formatting | bytes 8388608 | tf_op jit(solution)/shard_map/reshape | solution.py:119
  95.6 253.7 %while.27 = (s32[]{:T(128)}, bf16[8,64,16,128]{3,2,1,0:T(8,128)(2,1)}, bf16[512,16,128]{0,2,1:T(8,128)(2,1)}, bf16[512,16,128]{0,2,1:T(8,128)(2,1)}, f32[8,4,64,...) while((s32[]{:T(128)}, ...), condition=%wide.wide.region_11.12_spmd, body=%wide.wide.region_3.11_spmd.sunk | while | flops 72364288 | bytes 25006472 | solution.py:129
  98.2 3.3 copy.116
  101.6 3.5 copy.120
  105.2 20.9 %while.28 = (s32[]{:T(128)}, f32[4,16,64]{2,1,0:T(8,128)S(1)}, f32[4,16,64]{2,1,0:T(8,128)S(1)}, f32[64,16,4,32]{0,3,2,1:T(8,128)S(1)}, f32[4,128]{1,0:T(4,128)S...) while((s32[]{:T(128)}, f32[4,16,64]{2,1,0:T(8,128)S(1)}, ...), condition=%wide.region_10.10_spmd, body=%wide.region_4.9_spmd.sunk | while | flops 72102144 | bytes 9457287 | solution.py:81
  106.5 5.2 %conditional.2 = ((f32[4,16,64]{2,1,0:T(8,128)S(1)}, f32[4,16,64]{2,1,0:T(8,128)S(1)}, f32[64,16,4,32]{0,3,2,1:T(8,128)S(1)})) conditional(s32[]{:T(128)} %convert_element_type.97, (f32[4,16,64]{2,1,0:T(8,128)S(1)}, f32[4,16,64]{2,1,0:T(8,128)S(1)}, f32[64,16,4,32]{0,3,2,1:T(8,128)S(1)}) %tuple.69, (f32[1,128]{1,0:T(1,128)S(1)}, ...), branch_computations={%region_6.5_spmd, %region_7.8_spmd} | conditional | flops 72102016 | bytes 9456036 | solution.py:76
  114.4 5.2 %conditional.2 = ((f32[4,16,64]{2,1,0:T(8,128)S(1)}, f32[4,16,64]{2,1,0:T(8,128)S(1)}, f32[64,16,4,32]{0,3,2,1:T(8,128)S(1)})) conditional(s32[]{:T(128)} %convert_element_type.97, (f32[4,16,64]{2,1,0:T(8,128)S(1)}, f32[4,16,64]{2,1,0:T(8,128)S(1)}, f32[64,16,4,32]{0,3,2,1:T(8,128)S(1)}) %tuple.69, (f32[1,128]{1,0:T(1,128)S(1)}, ...), branch_computations={%region_6.5_spmd, %region_7.8_spmd} | conditional | flops 72102016 | bytes 9456036 | solution.py:76
  120.9 5.2 %conditional.2 = ((f32[4,16,64]{2,1,0:T(8,128)S(1)}, f32[4,16,64]{2,1,0:T(8,128)S(1)}, f32[64,16,4,32]{0,3,2,1:T(8,128)S(1)})) conditional(s32[]{:T(128)} %convert_element_type.97, (f32[4,16,64]{2,1,0:T(8,128)S(1)}, f32[4,16,64]{2,1,0:T(8,128)S(1)}, f32[64,16,4,32]{0,3,2,1:T(8,128)S(1)}) %tuple.69, (f32[1,128]{1,0:T(1,128)S(1)}, ...), branch_computations={%region_6.5_spmd, %region_7.8_spmd} | conditional | flops 72102016 | bytes 9456036 | solution.py:76
  130.0 3.3 copy.116
  133.3 3.5 copy.120
  136.9 20.9 %while.28 = (s32[]{:T(128)}, f32[4,16,64]{2,1,0:T(8,128)S(1)}, f32[4,16,64]{2,1,0:T(8,128)S(1)}, f32[64,16,4,32]{0,3,2,1:T(8,128)S(1)}, f32[4,128]{1,0:T(4,128)S...) while((s32[]{:T(128)}, f32[4,16,64]{2,1,0:T(8,128)S(1)}, ...), condition=%wide.region_10.10_spmd, body=%wide.region_4.9_spmd.sunk | while | flops 72102144 | bytes 9457287 | solution.py:81
  138.2 5.2 %conditional.2 = ((f32[4,16,64]{2,1,0:T(8,128)S(1)}, f32[4,16,64]{2,1,0:T(8,128)S(1)}, f32[64,16,4,32]{0,3,2,1:T(8,128)S(1)})) conditional(s32[]{:T(128)} %convert_element_type.97, (f32[4,16,64]{2,1,0:T(8,128)S(1)}, f32[4,16,64]{2,1,0:T(8,128)S(1)}, f32[64,16,4,32]{0,3,2,1:T(8,128)S(1)}) %tuple.69, (f32[1,128]{1,0:T(1,128)S(1)}, ...), branch_computations={%region_6.5_spmd, %region_7.8_spmd} | conditional | flops 72102016 | bytes 9456036 | solution.py:76
  146.1 5.2 %conditional.2 = ((f32[4,16,64]{2,1,0:T(8,128)S(1)}, f32[4,16,64]{2,1,0:T(8,128)S(1)}, f32[64,16,4,32]{0,3,2,1:T(8,128)S(1)})) conditional(s32[]{:T(128)} %convert_element_type.97, (f32[4,16,64]{2,1,0:T(8,128)S(1)}, f32[4,16,64]{2,1,0:T(8,128)S(1)}, f32[64,16,4,32]{0,3,2,1:T(8,128)S(1)}) %tuple.69, (f32[1,128]{1,0:T(1,128)S(1)}, ...), branch_computations={%region_6.5_spmd, %region_7.8_spmd} | conditional | flops 72102016 | bytes 9456036 | solution.py:76
  152.6 5.2 %conditional.2 = ((f32[4,16,64]{2,1,0:T(8,128)S(1)}, f32[4,16,64]{2,1,0:T(8,128)S(1)}, f32[64,16,4,32]{0,3,2,1:T(8,128)S(1)})) conditional(s32[]{:T(128)} %convert_element_type.97, (f32[4,16,64]{2,1,0:T(8,128)S(1)}, f32[4,16,64]{2,1,0:T(8,128)S(1)}, f32[64,16,4,32]{0,3,2,1:T(8,128)S(1)}) %tuple.69, (f32[1,128]{1,0:T(1,128)S(1)}, ...), branch_computations={%region_6.5_spmd, %region_7.8_spmd} | conditional | flops 72102016 | bytes 9456036 | solution.py:76
  161.7 3.3 copy.116
  165.0 3.5 copy.120
  168.6 20.9 %while.28 = (s32[]{:T(128)}, f32[4,16,64]{2,1,0:T(8,128)S(1)}, f32[4,16,64]{2,1,0:T(8,128)S(1)}, f32[64,16,4,32]{0,3,2,1:T(8,128)S(1)}, f32[4,128]{1,0:T(4,128)S...) while((s32[]{:T(128)}, f32[4,16,64]{2,1,0:T(8,128)S(1)}, ...), condition=%wide.region_10.10_spmd, body=%wide.region_4.9_spmd.sunk | while | flops 72102144 | bytes 9457287 | solution.py:81
  169.9 5.2 %conditional.2 = ((f32[4,16,64]{2,1,0:T(8,128)S(1)}, f32[4,16,64]{2,1,0:T(8,128)S(1)}, f32[64,16,4,32]{0,3,2,1:T(8,128)S(1)})) conditional(s32[]{:T(128)} %convert_element_type.97, (f32[4,16,64]{2,1,0:T(8,128)S(1)}, f32[4,16,64]{2,1,0:T(8,128)S(1)}, f32[64,16,4,32]{0,3,2,1:T(8,128)S(1)}) %tuple.69, (f32[1,128]{1,0:T(1,128)S(1)}, ...), branch_computations={%region_6.5_spmd, %region_7.8_spmd} | conditional | flops 72102016 | bytes 9456036 | solution.py:76
  177.8 5.2 %conditional.2 = ((f32[4,16,64]{2,1,0:T(8,128)S(1)}, f32[4,16,64]{2,1,0:T(8,128)S(1)}, f32[64,16,4,32]{0,3,2,1:T(8,128)S(1)})) conditional(s32[]{:T(128)} %convert_element_type.97, (f32[4,16,64]{2,1,0:T(8,128)S(1)}, f32[4,16,64]{2,1,0:T(8,128)S(1)}, f32[64,16,4,32]{0,3,2,1:T(8,128)S(1)}) %tuple.69, (f32[1,128]{1,0:T(1,128)S(1)}, ...), branch_computations={%region_6.5_spmd, %region_7.8_spmd} | conditional | flops 72102016 | bytes 9456036 | solution.py:76
  184.4 5.2 %conditional.2 = ((f32[4,16,64]{2,1,0:T(8,128)S(1)}, f32[4,16,64]{2,1,0:T(8,128)S(1)}, f32[64,16,4,32]{0,3,2,1:T(8,128)S(1)})) conditional(s32[]{:T(128)} %convert_element_type.97, (f32[4,16,64]{2,1,0:T(8,128)S(1)}, f32[4,16,64]{2,1,0:T(8,128)S(1)}, f32[64,16,4,32]{0,3,2,1:T(8,128)S(1)}) %tuple.69, (f32[1,128]{1,0:T(1,128)S(1)}, ...), branch_computations={%region_6.5_spmd, %region_7.8_spmd} | conditional | flops 72102016 | bytes 9456036 | solution.py:76
  193.4 3.3 copy.116
  196.7 3.5 copy.120
  200.3 20.9 %while.28 = (s32[]{:T(128)}, f32[4,16,64]{2,1,0:T(8,128)S(1)}, f32[4,16,64]{2,1,0:T(8,128)S(1)}, f32[64,16,4,32]{0,3,2,1:T(8,128)S(1)}, f32[4,128]{1,0:T(4,128)S...) while((s32[]{:T(128)}, f32[4,16,64]{2,1,0:T(8,128)S(1)}, ...), condition=%wide.region_10.10_spmd, body=%wide.region_4.9_spmd.sunk | while | flops 72102144 | bytes 9457287 | solution.py:81
  201.7 5.2 %conditional.2 = ((f32[4,16,64]{2,1,0:T(8,128)S(1)}, f32[4,16,64]{2,1,0:T(8,128)S(1)}, f32[64,16,4,32]{0,3,2,1:T(8,128)S(1)})) conditional(s32[]{:T(128)} %convert_element_type.97, (f32[4,16,64]{2,1,0:T(8,128)S(1)}, f32[4,16,64]{2,1,0:T(8,128)S(1)}, f32[64,16,4,32]{0,3,2,1:T(8,128)S(1)}) %tuple.69, (f32[1,128]{1,0:T(1,128)S(1)}, ...), branch_computations={%region_6.5_spmd, %region_7.8_spmd} | conditional | flops 72102016 | bytes 9456036 | solution.py:76
  209.5 5.2 %conditional.2 = ((f32[4,16,64]{2,1,0:T(8,128)S(1)}, f32[4,16,64]{2,1,0:T(8,128)S(1)}, f32[64,16,4,32]{0,3,2,1:T(8,128)S(1)})) conditional(s32[]{:T(128)} %convert_element_type.97, (f32[4,16,64]{2,1,0:T(8,128)S(1)}, f32[4,16,64]{2,1,0:T(8,128)S(1)}, f32[64,16,4,32]{0,3,2,1:T(8,128)S(1)}) %tuple.69, (f32[1,128]{1,0:T(1,128)S(1)}, ...), branch_computations={%region_6.5_spmd, %region_7.8_spmd} | conditional | flops 72102016 | bytes 9456036 | solution.py:76
  216.1 5.2 %conditional.2 = ((f32[4,16,64]{2,1,0:T(8,128)S(1)}, f32[4,16,64]{2,1,0:T(8,128)S(1)}, f32[64,16,4,32]{0,3,2,1:T(8,128)S(1)})) conditional(s32[]{:T(128)} %convert_element_type.97, (f32[4,16,64]{2,1,0:T(8,128)S(1)}, f32[4,16,64]{2,1,0:T(8,128)S(1)}, f32[64,16,4,32]{0,3,2,1:T(8,128)S(1)}) %tuple.69, (f32[1,128]{1,0:T(1,128)S(1)}, ...), branch_computations={%region_6.5_spmd, %region_7.8_spmd} | conditional | flops 72102016 | bytes 9456036 | solution.py:76
  225.1 3.3 copy.116
  228.4 3.5 copy.120
  232.0 20.9 %while.28 = (s32[]{:T(128)}, f32[4,16,64]{2,1,0:T(8,128)S(1)}, f32[4,16,64]{2,1,0:T(8,128)S(1)}, f32[64,16,4,32]{0,3,2,1:T(8,128)S(1)}, f32[4,128]{1,0:T(4,128)S...) while((s32[]{:T(128)}, f32[4,16,64]{2,1,0:T(8,128)S(1)}, ...), condition=%wide.region_10.10_spmd, body=%wide.region_4.9_spmd.sunk | while | flops 72102144 | bytes 9457287 | solution.py:81
  233.4 5.2 %conditional.2 = ((f32[4,16,64]{2,1,0:T(8,128)S(1)}, f32[4,16,64]{2,1,0:T(8,128)S(1)}, f32[64,16,4,32]{0,3,2,1:T(8,128)S(1)})) conditional(s32[]{:T(128)} %convert_element_type.97, (f32[4,16,64]{2,1,0:T(8,128)S(1)}, f32[4,16,64]{2,1,0:T(8,128)S(1)}, f32[64,16,4,32]{0,3,2,1:T(8,128)S(1)}) %tuple.69, (f32[1,128]{1,0:T(1,128)S(1)}, ...), branch_computations={%region_6.5_spmd, %region_7.8_spmd} | conditional | flops 72102016 | bytes 9456036 | solution.py:76
  241.3 5.2 %conditional.2 = ((f32[4,16,64]{2,1,0:T(8,128)S(1)}, f32[4,16,64]{2,1,0:T(8,128)S(1)}, f32[64,16,4,32]{0,3,2,1:T(8,128)S(1)})) conditional(s32[]{:T(128)} %convert_element_type.97, (f32[4,16,64]{2,1,0:T(8,128)S(1)}, f32[4,16,64]{2,1,0:T(8,128)S(1)}, f32[64,16,4,32]{0,3,2,1:T(8,128)S(1)}) %tuple.69, (f32[1,128]{1,0:T(1,128)S(1)}, ...), branch_computations={%region_6.5_spmd, %region_7.8_spmd} | conditional | flops 72102016 | bytes 9456036 | solution.py:76
  247.8 5.2 %conditional.2 = ((f32[4,16,64]{2,1,0:T(8,128)S(1)}, f32[4,16,64]{2,1,0:T(8,128)S(1)}, f32[64,16,4,32]{0,3,2,1:T(8,128)S(1)})) conditional(s32[]{:T(128)} %convert_element_type.97, (f32[4,16,64]{2,1,0:T(8,128)S(1)}, f32[4,16,64]{2,1,0:T(8,128)S(1)}, f32[64,16,4,32]{0,3,2,1:T(8,128)S(1)}) %tuple.69, (f32[1,128]{1,0:T(1,128)S(1)}, ...), branch_computations={%region_6.5_spmd, %region_7.8_spmd} | conditional | flops 72102016 | bytes 9456036 | solution.py:76
  256.8 3.3 copy.116
  260.1 3.5 copy.120
  263.8 20.9 %while.28 = (s32[]{:T(128)}, f32[4,16,64]{2,1,0:T(8,128)S(1)}, f32[4,16,64]{2,1,0:T(8,128)S(1)}, f32[64,16,4,32]{0,3,2,1:T(8,128)S(1)}, f32[4,128]{1,0:T(4,128)S...) while((s32[]{:T(128)}, f32[4,16,64]{2,1,0:T(8,128)S(1)}, ...), condition=%wide.region_10.10_spmd, body=%wide.region_4.9_spmd.sunk | while | flops 72102144 | bytes 9457287 | solution.py:81
  265.1 5.2 %conditional.2 = ((f32[4,16,64]{2,1,0:T(8,128)S(1)}, f32[4,16,64]{2,1,0:T(8,128)S(1)}, f32[64,16,4,32]{0,3,2,1:T(8,128)S(1)})) conditional(s32[]{:T(128)} %convert_element_type.97, (f32[4,16,64]{2,1,0:T(8,128)S(1)}, f32[4,16,64]{2,1,0:T(8,128)S(1)}, f32[64,16,4,32]{0,3,2,1:T(8,128)S(1)}) %tuple.69, (f32[1,128]{1,0:T(1,128)S(1)}, ...), branch_computations={%region_6.5_spmd, %region_7.8_spmd} | conditional | flops 72102016 | bytes 9456036 | solution.py:76
  273.0 5.2 %conditional.2 = ((f32[4,16,64]{2,1,0:T(8,128)S(1)}, f32[4,16,64]{2,1,0:T(8,128)S(1)}, f32[64,16,4,32]{0,3,2,1:T(8,128)S(1)})) conditional(s32[]{:T(128)} %convert_element_type.97, (f32[4,16,64]{2,1,0:T(8,128)S(1)}, f32[4,16,64]{2,1,0:T(8,128)S(1)}, f32[64,16,4,32]{0,3,2,1:T(8,128)S(1)}) %tuple.69, (f32[1,128]{1,0:T(1,128)S(1)}, ...), branch_computations={%region_6.5_spmd, %region_7.8_spmd} | conditional | flops 72102016 | bytes 9456036 | solution.py:76
  279.5 5.2 %conditional.2 = ((f32[4,16,64]{2,1,0:T(8,128)S(1)}, f32[4,16,64]{2,1,0:T(8,128)S(1)}, f32[64,16,4,32]{0,3,2,1:T(8,128)S(1)})) conditional(s32[]{:T(128)} %convert_element_type.97, (f32[4,16,64]{2,1,0:T(8,128)S(1)}, f32[4,16,64]{2,1,0:T(8,128)S(1)}, f32[64,16,4,32]{0,3,2,1:T(8,128)S(1)}) %tuple.69, (f32[1,128]{1,0:T(1,128)S(1)}, ...), branch_computations={%region_6.5_spmd, %region_7.8_spmd} | conditional | flops 72102016 | bytes 9456036 | solution.py:76
  288.5 3.3 copy.116
  291.9 3.5 copy.120
  295.5 20.9 %while.28 = (s32[]{:T(128)}, f32[4,16,64]{2,1,0:T(8,128)S(1)}, f32[4,16,64]{2,1,0:T(8,128)S(1)}, f32[64,16,4,32]{0,3,2,1:T(8,128)S(1)}, f32[4,128]{1,0:T(4,128)S...) while((s32[]{:T(128)}, f32[4,16,64]{2,1,0:T(8,128)S(1)}, ...), condition=%wide.region_10.10_spmd, body=%wide.region_4.9_spmd.sunk | while | flops 72102144 | bytes 9457287 | solution.py:81
  296.8 5.2 %conditional.2 = ((f32[4,16,64]{2,1,0:T(8,128)S(1)}, f32[4,16,64]{2,1,0:T(8,128)S(1)}, f32[64,16,4,32]{0,3,2,1:T(8,128)S(1)})) conditional(s32[]{:T(128)} %convert_element_type.97, (f32[4,16,64]{2,1,0:T(8,128)S(1)}, f32[4,16,64]{2,1,0:T(8,128)S(1)}, f32[64,16,4,32]{0,3,2,1:T(8,128)S(1)}) %tuple.69, (f32[1,128]{1,0:T(1,128)S(1)}, ...), branch_computations={%region_6.5_spmd, %region_7.8_spmd} | conditional | flops 72102016 | bytes 9456036 | solution.py:76
  304.7 5.2 %conditional.2 = ((f32[4,16,64]{2,1,0:T(8,128)S(1)}, f32[4,16,64]{2,1,0:T(8,128)S(1)}, f32[64,16,4,32]{0,3,2,1:T(8,128)S(1)})) conditional(s32[]{:T(128)} %convert_element_type.97, (f32[4,16,64]{2,1,0:T(8,128)S(1)}, f32[4,16,64]{2,1,0:T(8,128)S(1)}, f32[64,16,4,32]{0,3,2,1:T(8,128)S(1)}) %tuple.69, (f32[1,128]{1,0:T(1,128)S(1)}, ...), branch_computations={%region_6.5_spmd, %region_7.8_spmd} | conditional | flops 72102016 | bytes 9456036 | solution.py:76
  311.2 5.2 %conditional.2 = ((f32[4,16,64]{2,1,0:T(8,128)S(1)}, f32[4,16,64]{2,1,0:T(8,128)S(1)}, f32[64,16,4,32]{0,3,2,1:T(8,128)S(1)})) conditional(s32[]{:T(128)} %convert_element_type.97, (f32[4,16,64]{2,1,0:T(8,128)S(1)}, f32[4,16,64]{2,1,0:T(8,128)S(1)}, f32[64,16,4,32]{0,3,2,1:T(8,128)S(1)}) %tuple.69, (f32[1,128]{1,0:T(1,128)S(1)}, ...), branch_computations={%region_6.5_spmd, %region_7.8_spmd} | conditional | flops 72102016 | bytes 9456036 | solution.py:76
  320.2 3.3 copy.116
  323.6 3.5 copy.120
  327.2 20.9 %while.28 = (s32[]{:T(128)}, f32[4,16,64]{2,1,0:T(8,128)S(1)}, f32[4,16,64]{2,1,0:T(8,128)S(1)}, f32[64,16,4,32]{0,3,2,1:T(8,128)S(1)}, f32[4,128]{1,0:T(4,128)S...) while((s32[]{:T(128)}, f32[4,16,64]{2,1,0:T(8,128)S(1)}, ...), condition=%wide.region_10.10_spmd, body=%wide.region_4.9_spmd.sunk | while | flops 72102144 | bytes 9457287 | solution.py:81
  328.5 5.2 %conditional.2 = ((f32[4,16,64]{2,1,0:T(8,128)S(1)}, f32[4,16,64]{2,1,0:T(8,128)S(1)}, f32[64,16,4,32]{0,3,2,1:T(8,128)S(1)})) conditional(s32[]{:T(128)} %convert_element_type.97, (f32[4,16,64]{2,1,0:T(8,128)S(1)}, f32[4,16,64]{2,1,0:T(8,128)S(1)}, f32[64,16,4,32]{0,3,2,1:T(8,128)S(1)}) %tuple.69, (f32[1,128]{1,0:T(1,128)S(1)}, ...), branch_computations={%region_6.5_spmd, %region_7.8_spmd} | conditional | flops 72102016 | bytes 9456036 | solution.py:76
  336.4 5.2 %conditional.2 = ((f32[4,16,64]{2,1,0:T(8,128)S(1)}, f32[4,16,64]{2,1,0:T(8,128)S(1)}, f32[64,16,4,32]{0,3,2,1:T(8,128)S(1)})) conditional(s32[]{:T(128)} %convert_element_type.97, (f32[4,16,64]{2,1,0:T(8,128)S(1)}, f32[4,16,64]{2,1,0:T(8,128)S(1)}, f32[64,16,4,32]{0,3,2,1:T(8,128)S(1)}) %tuple.69, (f32[1,128]{1,0:T(1,128)S(1)}, ...), branch_computations={%region_6.5_spmd, %region_7.8_spmd} | conditional | flops 72102016 | bytes 9456036 | solution.py:76
  342.9 5.2 %conditional.2 = ((f32[4,16,64]{2,1,0:T(8,128)S(1)}, f32[4,16,64]{2,1,0:T(8,128)S(1)}, f32[64,16,4,32]{0,3,2,1:T(8,128)S(1)})) conditional(s32[]{:T(128)} %convert_element_type.97, (f32[4,16,64]{2,1,0:T(8,128)S(1)}, f32[4,16,64]{2,1,0:T(8,128)S(1)}, f32[64,16,4,32]{0,3,2,1:T(8,128)S(1)}) %tuple.69, (f32[1,128]{1,0:T(1,128)S(1)}, ...), branch_computations={%region_6.5_spmd, %region_7.8_spmd} | conditional | flops 72102016 | bytes 9456036 | solution.py:76
  349.3 3.8 all-to-all-start.1
  353.4 24.0 %all-to-all-done.1 = bf16[512,16,128]{2,1,0:T(8,128)(2,1)S(1)} async-done(((bf16[512,16,128]{2,1,0:T(8,128)(2,1)}), bf16[512,16,128]{2,1,0:T(8,128)(2,1)S(1)}, u32[]{:S(2)}, u32[]{:S(2)}) %all-to-all-start.1) | async-done | bytes 2097184 | tf_op jit(solution)/shard_map/all_to_all | solution.py:131
  380.4 8.5 %fusion.20 = bf16[128,64,128]{2,0,1:T(8,128)(2,1)} fusion(f32[128,64]{0,1:T(8,128)S(1)} %broadcast_multiply_fusion, f32[128]{0:T(128)S(1)} %copy-done.10, bf16[128,64,128]{2,1,0:T(8,128)(2,1)S(1)} %copy-done.2, f32[128,64,128]{2,1,0:T(8,128)} %bitcast.101, bf16[128,64,128]{2,0,1:T(8,128)(2,1)} %copy-done.3, f32[128]{0:T(128)S(1)} %copy-done.11, ...), kind=kOutput, calls=%fused_computation.35 | convolution fusion | flops 548405248 | bytes 10585088 | tf_op jit(solution)/shard_map/dot_general | solution.py:136
  388.9 4.3 %copy.85 = bf16[128,64,128]{2,1,0:T(8,128)(2,1)} copy(bf16[128,64,128]{2,0,1:T(8,128)(2,1)} %fusion.20) | data formatting | bytes 4194304 | tf_op jit(solution)/shard_map/convert_element_type | solution.py:143
  (403 shorter events, 190.0 us)
Async XLA Ops:
  6.5 373.9 %copy-start = (bf16[128,128]{1,0:T(8,128)(2,1)S(1)}, bf16[128,128]{1,0:T(8,128)(2,1)}, u32[]{:S(2)}) copy-start(bf16[128,128]{1,0:T(8,128)(2,1)} %param.21) | copy-start | bytes 98308
  6.5 3.6 copy-start.1
  6.5 9.7 %copy-start.8 = (f32[128]{0:T(128)S(1)}, f32[128]{0:T(128)}, u32[]{:S(2)}) copy-start(f32[128]{0:T(128)} %param.16) | copy-start | bytes 1540
  6.5 9.7 %copy-start.7 = (f32[128]{0:T(128)S(1)}, f32[128]{0:T(128)}, u32[]{:S(2)}) copy-start(f32[128]{0:T(128)} %param.17) | copy-start | bytes 1540
  6.5 83.7 %all-gather.2.cloned.1.call-start = ((), (), s32[]{:S(2)}) async-start(), calls=%async_computation.2 | async-start | bytes 4718592 | tf_op jit(solution)/shard_map/all_gather | solution.py:112
  16.3 6.3 %copy-start.6 = (bf16[128,4]{0,1:T(4,128)(2,1)S(1)}, bf16[128,4]{0,1:T(4,128)(2,1)}, u32[]{:S(2)}) copy-start(bf16[128,4]{0,1:T(4,128)(2,1)} %param.20) | copy-start | bytes 3076
  21.2 1.3 copy-start.3
  35.5 3.8 copy-start.9
  35.5 27.0 %all-to-all-start = ((bf16[128,64,128]{2,0,1:T(8,128)(2,1)}), bf16[128,64,128]{2,0,1:T(8,128)(2,1)S(1)}, u32[]{:S(2)}, u32[]{:S(2)}) async-start(bf16[128,64,128]{2,0,1:T(8,128)(2,1)} %copy-done.3), calls=%async_computation | async-start | bytes 4194304 | tf_op jit(solution)/shard_map/all_to_all | solution.py:101
  62.5 0.9 copy-start.5
  75.8 2.3 copy-start.4
  349.3 28.1 %all-to-all-start.1 = ((bf16[512,16,128]{2,1,0:T(8,128)(2,1)}), bf16[512,16,128]{2,1,0:T(8,128)(2,1)S(1)}, u32[]{:S(2)}, u32[]{:S(2)}) async-start(bf16[512,16,128]{2,1,0:T(8,128)(2,1)} %bitcast.102), calls=%async_computation.1 | async-start | bytes 4194304 | tf_op jit(solution)/shard_map/all_to_all | solution.py:131
  377.8 2.6 copy-start.2
  377.8 2.6 copy-start.10
  377.8 2.6 copy-start.11
Sparse Core Ops, SparseCore 0:
  35.6 47.1 all-gather.1
where the time goes:
time: 404 us; the launch traced here: 400 us
  local copies, waits for them, and re-layouts  116 us (29%)
  matrix products  104 us (26%)
  other arithmetic  75.2 us (19%)
  waiting for transfers between devices  47.1 us (12%)
  loops' own time  24.1 us (6%)
  between operations  13.6 us (3%)
  blocking collectives  12.3 us (3%)
  starting transfers between devices  7.66 us (2%)
    while x32, local copies, waits for them, and re-layouts, fold_keys(): lax.scan(scan_step, carried, (key_blocks, value_blocks, bias_blocks, mask...  55.1 us
    dot_general x24, matrix products, update(): jnp.einsum('ijhd,kjhd->hjik', query_heads, key_part, preferred_element_ty...  47.1 us
    dot_general x24, matrix products, update(): jnp.einsum('hjik,kjhd->ijhd', weights.astype(jnp.bfloat16), value_part, p...  41.5 us
    convert_element_type x24, other arithmetic, update(): weights.astype(jnp.bfloat16)  32.2 us
    all_to_all x1, waiting for transfers between devices, shards(): lax.all_to_all(gathered, 'row', split_axis=0, concat_axis=1, tiled=True)  24 us
    all_to_all x1, waiting for transfers between devices, shards(): lax.all_to_all(normed, 'row', split_axis=1, concat_axis=0, tiled=True)  23.1 us
    reduce_max x32, other arithmetic, scan_step(): jnp.max(operands[3]) > 0  21.5 us
    another operation x8, loops' own time, fold_keys(): lax.scan(scan_step, carried, (key_blocks, value_blocks, bias_blocks, mask...  21.4 us
  transfers between devices with their start and end apart: 3, of which 2 were waited for; matrix products, arithmetic and copies ran while one was open for 7% of the time, Pallas kernels for 0%

commit v1 on v0

v1 whole, which is shorter than its diff:
```python
import functools

import jax
import jax.numpy as jnp
from jax import lax
from jax.experimental import pallas as pl
from jax.experimental.pallas import tpu as pltpu
from jax.sharding import PartitionSpec as P

H = 4
HD = 32
NT = (((1,), (1,)), ((), ()))


def norm_kernel(pair_ref, gain_ref, shift_ref, wb_ref, normed_ref, bias_ref, held):
    rows, step_j, channels = pair_ref.shape
    flat = pair_ref[...].astype(jnp.float32).reshape(rows * step_j, channels)
    average = jnp.mean(flat, axis=-1, keepdims=True)
    centred = flat - average
    spread = jnp.mean(centred * centred, axis=-1, keepdims=True)
    held[...] = centred * lax.rsqrt(spread + 1e-05) * gain_ref[...] + shift_ref[...]
    for j in range(step_j):
        column = held[pl.ds(j, rows, stride=step_j), :].astype(jnp.bfloat16)
        normed_ref[j] = column
        part = lax.dot_general(wb_ref[...], column, NT, preferred_element_type=jnp.float32)
        for h in range(H):
            bias_ref[h, j : j + 1, :] = part[h : h + 1, :]


def attend_kernel(
    flags_ref, x_ref, w_ref, gb_ref, bias_ref, out_ref, order, q4, keys, vext, gates
):
    slots, _, rows, channels = x_ref.shape
    inner = H * HD
    tiles = rows // bias_ref.shape[3]
    count = jnp.int32(0)
    for b in range(slots):
        order[count] = b
        count = count + flags_ref[b]
    lane = lax.broadcasted_iota(jnp.int32, (rows, inner), 1) // HD

    def project(s, carry):
        x = x_ref[order[s], 0]
        proj = jnp.dot(x, w_ref[...], preferred_element_type=jnp.float32)
        q = proj[:, :inner] * HD ** (-0.5)
        for h in range(H):
            q4[s, h] = jnp.where(lane == h, q, 0.0).astype(jnp.bfloat16)
        at = pl.ds(pl.multiple_of(s * rows, rows), rows)
        keys[at, :] = proj[:, inner : 2 * inner].astype(jnp.bfloat16)
        vext[at, :inner] = proj[:, 2 * inner : 3 * inner].astype(jnp.bfloat16)
        vext[at, inner:] = jnp.ones((rows, inner), jnp.bfloat16)
        gates[s] = jax.nn.sigmoid(proj[:, 3 * inner :] + gb_ref[...])
        return carry

    wanted = count * flags_ref[slots]
    lax.fori_loop(0, wanted, project, 0)

    def queries(n):
        def body(s, carry):
            block = order[s]
            top = jnp.zeros((rows, inner), jnp.float32)
            low = jnp.ones((rows, inner), jnp.float32)
            for h in range(H):
                scores = lax.dot_general(
                    q4[s, h], keys[: n * rows, :], NT, preferred_element_type=jnp.float32
                )
                parts = [
                    bias_ref[order[t], pl.ds(block * tiles, tiles), h].reshape(rows, rows)
                    for t in range(n)
                ]
                scores = scores + jnp.concatenate(parts, axis=1)
                peak = jnp.max(scores, axis=-1, keepdims=True)
                weights = jnp.exp(scores - peak).astype(jnp.bfloat16)
                mixed = jnp.dot(weights, vext[: n * rows, :], preferred_element_type=jnp.float32)
                top = jnp.where(lane == h, mixed[:, :inner], top)
                low = jnp.where(lane == h, mixed[:, inner:], low)
            attended = (top / low).astype(jnp.bfloat16).astype(jnp.float32)
            out_ref[block, 0] = (gates[s] * attended).astype(jnp.bfloat16)
            return carry

        lax.fori_loop(0, wanted, body, 0)

    for n in range(1, keys.shape[0] // rows + 1):
        pl.when(count == n)(functools.partial(queries, n))


def close_kernel(flags_ref, gated_ref, pair_ref, w_ref, ob_ref, out_ref, held):
    cols, step_i, inner = gated_ref.shape

    @pl.when(flags_ref[0] > 0)
    def _():
        flat = gated_ref[...].reshape(cols * step_i, inner)
        held[...] = jnp.dot(flat, w_ref[...], preferred_element_type=jnp.float32) + ob_ref[...]
        for i in range(step_i):
            update = held[pl.ds(i, cols, stride=step_i), :]
            out_ref[i] = (pair_ref[i].astype(jnp.float32) + update).astype(jnp.bfloat16)

    @pl.when(flags_ref[0] == 0)
    def _():
        out_ref[...] = pair_ref[...]


def shards(pair_rep, ln_gain, ln_shift, w_proj, gate_bias, w_bias, w_out, out_bias, block_valid):
    rows, cols, channels = pair_rep.shape
    row_count = lax.axis_size("row")
    col_count = lax.axis_size("col")
    row_id = lax.axis_index("row")
    col_id = lax.axis_index("col")
    inner = H * HD
    width = cols // row_count
    blocks = block_valid.shape[0]
    block_width = rows * row_count // blocks
    assert block_width % rows == 0 and block_width % cols == 0 and rows % cols == 0
    most = row_count - block_width // rows
    smem = pl.BlockSpec(memory_space=pltpu.SMEM)

    def whole(*shape):
        return pl.BlockSpec(shape, lambda g: (0,) * len(shape))

    present = (block_valid > 0).astype(jnp.int32)
    per_slot = jnp.repeat(present, row_count // blocks) if row_count != blocks else present
    col_ok = present[col_id * cols // block_width]
    row_ok = present[row_id * rows // block_width]
    flags = jnp.concatenate([per_slot, col_ok[None]])
    own = (col_ok * row_ok)[None]

    step_j = 16 if cols % 16 == 0 else cols
    normed, bias_local = pl.pallas_call(
        norm_kernel,
        grid=(cols // step_j,),
        in_specs=[
            pl.BlockSpec((rows, step_j, channels), lambda g: (0, g, 0)),
            whole(1, channels),
            whole(1, channels),
            whole(H, channels),
        ],
        out_specs=[
            pl.BlockSpec((step_j, rows, channels), lambda g: (g, 0, 0)),
            pl.BlockSpec((H, step_j, rows), lambda g: (0, g, 0)),
        ],
        out_shape=[
            jax.ShapeDtypeStruct((cols, rows, channels), jnp.bfloat16),
            jax.ShapeDtypeStruct((H, cols, rows), jnp.float32),
        ],
        scratch_shapes=[pltpu.VMEM((rows * step_j, channels), jnp.float32)],
        name="norm",
    )(pair_rep, ln_gain[None], ln_shift[None], w_bias.T)

    bias = lax.all_gather(bias_local, ("row", "col"), axis=0)
    bias = bias.reshape(row_count, col_count, H, cols, rows)
    x = lax.all_to_all(
        normed.reshape(row_count, width, rows, channels), "row", 0, 0, tiled=True
    )
    gated = pl.pallas_call(
        attend_kernel,
        grid=(width,),
        in_specs=[
            smem,
            pl.BlockSpec((row_count, 1, rows, channels), lambda g: (0, g, 0, 0)),
            whole(channels, 4 * inner),
            whole(1, inner),
            pl.BlockSpec(
                (row_count, col_count, H, cols, rows),
                lambda g: (0, 0, 0, 0, 0),
                pipeline_mode=pl.Buffered(1),
            ),
        ],
        out_specs=pl.BlockSpec((row_count, 1, rows, inner), lambda g: (0, g, 0, 0)),
        out_shape=jax.ShapeDtypeStruct((row_count, width, rows, inner), jnp.bfloat16),
        scratch_shapes=[
            pltpu.SMEM((row_count + 1,), jnp.int32),
            pltpu.VMEM((most, H, rows, inner), jnp.bfloat16),
            pltpu.VMEM((most * rows, inner), jnp.bfloat16),
            pltpu.VMEM((most * rows, 2 * inner), jnp.bfloat16),
            pltpu.VMEM((most, rows, inner), jnp.float32),
        ],
        name="attend",
    )(flags, x, w_proj, gate_bias[None], bias)
    gated = lax.all_to_all(gated, "row", 0, 0, tiled=True)

    step_i = 32 if rows % 32 == 0 else rows
    return pl.pallas_call(
        close_kernel,
        grid=(rows // step_i,),
        in_specs=[
            smem,
            pl.BlockSpec((cols, step_i, inner), lambda g: (0, g, 0)),
            pl.BlockSpec((step_i, cols, channels), lambda g: (g, 0, 0)),
            whole(inner, channels),
            whole(1, channels),
        ],
        out_specs=pl.BlockSpec((step_i, cols, channels), lambda g: (g, 0, 0)),
        out_shape=jax.ShapeDtypeStruct((rows, cols, channels), jnp.bfloat16),
        scratch_shapes=[pltpu.VMEM((cols * step_i, channels), jnp.float32)],
        name="close",
    )(own, gated.reshape(cols, rows, inner), pair_rep, w_out, out_bias[None])


def solution(mesh):
    return jax.shard_map(
        shards,
        mesh=mesh,
        in_specs=(P("row", "col", None), P(), P(), P(), P(), P(), P(), P(), P()),
        out_specs=P("row", "col", None),
        check_vma=False,
    )
```

time: 404 us -> 173 us (0.43)
  local copies, waits for them, and re-layouts: 116 us -> 2 us
  matrix products: 104 us -> 0 us
  other arithmetic: 75.2 us -> 1.3 us
  Pallas kernels: 0 us -> 58.1 us
  waiting for transfers between devices: 47.1 us -> 87.1 us
  loops' own time: 24.1 us -> 0 us
  blocking collectives: 12.3 us -> 0 us
    dot_general x51 -> x0, matrix products: 104 us -> none  [the longest x24 47.1 us: update(): jnp.einsum('ijhd,kjhd->hjik', query_heads, key_part, preferred_element_ty...]
    while x34 -> x0, local copies, waits for them, and re-layouts: 61.8 us -> none  [the longest x32 55.1 us: fold_keys(): lax.scan(scan_step, carried, (key_blocks, value_blocks, bias_blocks, mask...]
    pallas_call x0 -> x3, Pallas kernels: none -> 58.1 us  [the longest x1 45.4 us: shards(): pl.pallas_call(attend_kernel, grid=(width,), in_specs=[smem, pl.BlockSpec...]
    convert_element_type x36 -> x1, other arithmetic: 42.9 us -> 0.01 us  [shards(): present = (block_valid > 0).astype(jnp.int32)]
    all_gather x1, waiting for transfers between devices: 0.01 us -> 39 us  [shards(): bias = lax.all_gather(bias_local, ('row', 'col'), axis=0)]
    another operation x41 -> x0, loops' own time: 24.1 us -> none  [the longest x8 21.4 us: fold_keys(): lax.scan(scan_step, carried, (key_blocks, value_blocks, bias_blocks, mask...]
    reduce_max x32 -> x0, other arithmetic: 21.5 us -> none  [scan_step(): jnp.max(operands[3]) > 0]
    dynamic_slice x26 -> x1, local copies, waits for them, and re-layouts: 18.9 us -> 0.66 us  [shards(): row_ok = present[row_id * rows // block_width]]
  transfers between devices with their start and end apart: 3 -> 3, of which waited for: 2 -> 3; matrix products, arithmetic and copies ran while one was open for 7% -> 1% of each run, Pallas kernels for 0% -> 0%
where the time goes in v1:
time: 173 us; the launch traced here: 172 us
  waiting for transfers between devices  87.1 us (50%)
  Pallas kernels  58.1 us (34%)
  between operations  14.7 us (8%)
  starting transfers between devices  8.81 us (5%)
  local copies, waits for them, and re-layouts  2 us (1%)
    pallas_call x1, Pallas kernels, shards(): pl.pallas_call(attend_kernel, grid=(width,), in_specs=[smem, pl.BlockSpec...  45.4 us
    all_gather x1, waiting for transfers between devices, shards(): bias = lax.all_gather(bias_local, ('row', 'col'), axis=0)  39 us
    all_to_all x1, waiting for transfers between devices, shards(): gated = lax.all_to_all(gated, 'row', 0, 0, tiled=True)  24.3 us
    all_to_all x1, waiting for transfers between devices, shards(): lax.all_to_all(normed.reshape(row_count, width, rows, channels), 'row', 0...  23.8 us
    pallas_call x1, Pallas kernels, shards(): pl.pallas_call(close_kernel, grid=(rows // step_i,), in_specs=[smem, pl.B...  6.81 us
    pallas_call x1, Pallas kernels, shards(): pl.pallas_call(norm_kernel, grid=(cols // step_j,), in_specs=[pl.BlockSpe...  5.87 us
    all_to_all x1, starting transfers between devices, shards(): lax.all_to_all(normed.reshape(row_count, width, rows, channels), 'row', 0...  5.2 us
    all_to_all x1, starting transfers between devices, shards(): gated = lax.all_to_all(gated, 'row', 0, 0, tiled=True)  3.61 us
  transfers between devices with their start and end apart: 3, of which 3 were waited for; matrix products, arithmetic and copies ran while one was open for 1% of the time, Pallas kernels for 0%

profile of v1, /device:TPU:0, one launch (start us, length us, event | category | flops | bytes accessed | tf_op | source)
XLA Modules:
  0.0 172.0 jit_solution(2027541482440105522)
XLA Ops:
  6.5 0.0 all-gather.3.cloned.1.call-start
  6.5 5.9 %norm.1 = (bf16[64,128,128]{2,1,0:T(8,128)(2,1)}, f32[4,64,128]{2,1,0:T(8,128)}) custom-call(bf16[128,64,128]{2,1,0:T(8,128)(2,1)} %pair_ref.3, f32[1,128]{1,0:T(1,128)} %bitcast.12, f32[1,128]{1,0:T(1,128)} %bitcast.13, bf16[4,128]{1,0:T(4,128)(2,1)} %bitcast.11), custom_call_target="tpu_custom_call" | custom-call | tf_op jit(solution)/shard_map/norm/pallas_call | solution.py:128
  12.4 0.0 all-gather.3.cloned.1.call-update
  12.4 0.0 copy-start.2
  12.4 5.2 %all-to-all-start = ((bf16[4,16,128,128]{3,2,1,0:T(8,128)(2,1)}), bf16[4,16,128,128]{3,2,1,0:T(8,128)(2,1)S(1)}, u32[]{:S(2)}, u32[]{:S(2)}) async-start(bf16[4,16,128,128]{3,2,1,0:T(8,128)(2,1)} %bitcast.10), calls=%async_computation | async-start | bytes 4194304 | tf_op jit(solution)/shard_map/all_to_all | solution.py:151
  17.6 0.0 copy-done.2
  17.7 0.7 fusion
  18.3 1.3 pad_add_fusion.flags_ref
  19.6 23.8 %all-to-all-done.x_ref = bf16[4,16,128,128]{3,2,1,0:T(8,128)(2,1)S(1)} async-done(((bf16[4,16,128,128]{3,2,1,0:T(8,128)(2,1)}), bf16[4,16,128,128]{3,2,1,0:T(8,128)(2,1)S(1)}, u32[]{:S(2)}, u32[]{:S(2)}) %all-to-all-start) | async-done | bytes 2097184 | tf_op jit(solution)/shard_map/all_to_all | solution.py:151
  43.5 0.0 copy-start
  43.5 39.0 %all-gather.3.cloned.1.call-done = f32[128,64,128]{2,1,0:T(8,128)} async-done(((f32[4,64,128]{2,1,0:T(8,128)}), f32[128,64,128]{2,1,0:T(8,128)}) %all-gather.3.cloned.1.call-update) | async-done | bytes 4194320 | tf_op jit(solution)/shard_map/all_gather | solution.py:149
  82.5 0.0 copy-done
  82.5 45.4 %attend.1 = bf16[4,16,128,128]{3,2,1,0:T(8,128)(2,1)} custom-call(s32[5]{0:T(128)} %pad_add_fusion.flags_ref, bf16[4,16,128,128]{3,2,1,0:T(8,128)(2,1)} %copy-done, bf16[128,512]{1,0:T(8,128)(2,1)} %w_ref.2, f32[1,128]{1,0:T(1,128)} %bitcast.14, f32[4,8,4,64,128]{4,3,2,1,0:T(8,128)} %bitcast.9), custom_call_target="tpu_custom_call" | custom-call | tf_op jit(solution)/shard_map/attend/pallas_call | solution.py:154
  127.9 3.6 %all-to-all-start.1 = ((bf16[4,16,128,128]{3,2,1,0:T(8,128)(2,1)}), bf16[4,16,128,128]{3,2,1,0:T(8,128)(2,1)S(1)}, u32[]{:S(2)}, u32[]{:S(2)}) async-start(bf16[4,16,128,128]{3,2,1,0:T(8,128)(2,1)} %attend.1), calls=%async_computation.1 | async-start | bytes 4194304 | tf_op jit(solution)/shard_map/all_to_all | solution.py:179
  132.7 24.3 %all-to-all-done.1 = bf16[4,16,128,128]{3,2,1,0:T(8,128)(2,1)S(1)} async-done(((bf16[4,16,128,128]{3,2,1,0:T(8,128)(2,1)}), bf16[4,16,128,128]{3,2,1,0:T(8,128)(2,1)S(1)}, u32[]{:S(2)}, u32[]{:S(2)}) %all-to-all-start.1) | async-done | bytes 2097184 | tf_op jit(solution)/shard_map/all_to_all | solution.py:179
  157.0 0.0 copy-start.1
  157.0 1.3 copy-done.1
  158.3 6.8 %close.1 = bf16[128,64,128]{2,1,0:T(8,128)(2,1)} custom-call(s32[1]{0:T(128)S(6)} %mul.12.flags_ref, bf16[64,128,128]{2,1,0:T(8,128)(2,1)} %bitcast.8, bf16[128,64,128]{2,1,0:T(8,128)(2,1)} %pair_ref.3, bf16[128,128]{1,0:T(8,128)(2,1)} %w_ref.3, f32[1,128]{1,0:T(1,128)} %bitcast.15), custom_call_target="tpu_custom_call" | custom-call | tf_op jit(solution)/shard_map/close/pallas_call | solution.py:182
  (1 shorter events, 0.0 us)
Async XLA Ops:
  6.5 75.9 %all-gather.3.cloned.1.call-start = ((), (), s32[]{:S(2)}) async-start(), calls=%async_computation.2 | async-start | bytes 4325376 | tf_op jit(solution)/shard_map/all_gather | solution.py:149
  12.4 5.2 %copy-start.2 = (s32[4]{0:T(128)S(1)}, s32[4]{0:T(128)}, u32[]{:S(2)}) copy-start(s32[4]{0:T(128)} %param.17) | copy-start | bytes 52
  12.4 31.0 %all-to-all-start = ((bf16[4,16,128,128]{3,2,1,0:T(8,128)(2,1)}), bf16[4,16,128,128]{3,2,1,0:T(8,128)(2,1)S(1)}, u32[]{:S(2)}, u32[]{:S(2)}) async-start(bf16[4,16,128,128]{3,2,1,0:T(8,128)(2,1)} %bitcast.10), calls=%async_computation | async-start | bytes 4194304 | tf_op jit(solution)/shard_map/all_to_all | solution.py:151
  43.5 39.0 %copy-start = (bf16[4,16,128,128]{3,2,1,0:T(8,128)(2,1)}, bf16[4,16,128,128]{3,2,1,0:T(8,128)(2,1)S(1)}, u32[]{:S(2)}) copy-start(bf16[4,16,128,128]{3,2,1,0:T(8,128)(2,1)S(1)} %all-to-all-done.x_ref) | copy-start | bytes 6291460
  127.9 29.1 %all-to-all-start.1 = ((bf16[4,16,128,128]{3,2,1,0:T(8,128)(2,1)}), bf16[4,16,128,128]{3,2,1,0:T(8,128)(2,1)S(1)}, u32[]{:S(2)}, u32[]{:S(2)}) async-start(bf16[4,16,128,128]{3,2,1,0:T(8,128)(2,1)} %attend.1), calls=%async_computation.1 | async-start | bytes 4194304 | tf_op jit(solution)/shard_map/all_to_all | solution.py:179
  157.0 1.3 copy-start.1
Sparse Core Ops, SparseCore 0:
  12.6 69.8 all-gather.2
